TPU v7x, 32 devices: a whole 2x2x4 slice. The times are simulated.
32 devices in a mesh: row: 4 (over x, core), col: 8 (over z, y).
Axes of the slice: x: 2, y: 2, z: 4, core: 2. Of those that a mesh axis runs over, the one named last changes fastest.
Arguments:
- matrix: float32 [2048, 2048], P('row', 'col'), as said below
- start_vectors: float32 [2048, 512], P(('col', 'row')), may hold values from -6 to 6
- interval: float32 [2], replicated, as said below
Outputs:
- ortho_basis: float32 [2048, 512], P(('col', 'row'))
- projected: float32 [512, 512], replicated
- residual: float32 [2048, 512], P(('col', 'row'))
Inputs may be any that keep to these rules, and one draw needn't show every extreme that they name: matrix is exactly symmetric (entry (r, c) equals entry (c, r)); its eigenvalues lie within about -1.45 to 1.45. interval[0] lies in [-1.2, -0.7] and interval[1] in [1.45, 1.9].
All inputs are finite; a program needn't handle non-finite values.
Results may differ from a plain program's by a relative error of at most 0.0003.
Values sent between devices are 32-bit elements.
A program may use at most 128 MiB of HBM per device.

v0:
```python
import jax
import jax.numpy as jnp
from jax import lax
from jax.sharding import PartitionSpec as P

FILTER_DEG = 3
OUTER = 2


def scattered(contribution, width, axis):
    whole = contribution(jnp.int32(0), width * lax.axis_size(axis))
    return lax.psum_scatter(whole, axis, scatter_dimension=0, tiled=True)


def spread(array, axis, root):
    mine = lax.axis_index(axis) == root
    return lax.psum(jnp.where(mine, array, jnp.zeros_like(array)), axis)


def product(left, right):
    return jnp.dot(left, right, precision=lax.Precision.HIGHEST, preferred_element_type=jnp.float32)


def tri_solve(factor, values):
    return jax.scipy.linalg.solve_triangular(factor, values, lower=True)


def on_device(matrix, start_vectors, interval):
    block_rows, block_cols = matrix.shape
    slab_rows = start_vectors.shape[0]
    total_rows = slab_rows * lax.axis_size("row") * lax.axis_size("col")
    row_index = lax.axis_index("row")
    col_index = lax.axis_index("col")
    center = 0.5 * (interval[0] + interval[1])
    half_width = 0.5 * (interval[1] - interval[0])
    global_rows = row_index * block_rows + lax.iota(jnp.int32, block_rows)
    global_cols = col_index * block_cols + lax.iota(jnp.int32, block_cols)
    diagonal = global_rows[:, None] == global_cols[None, :]
    shifted = jnp.where(diagonal, matrix - center, matrix) / half_width

    def forward(col_full):

        def term(first_row, row_count):
            strip = lax.dynamic_slice_in_dim(shifted, first_row, row_count, 0)
            return product(strip, col_full)

        return scattered(term, slab_rows, "col")

    def gather_rows(slab_part):
        return lax.all_gather(slab_part, "col", axis=0, tiled=True)

    def to_columns(row_full):
        root_row = col_index * block_cols // block_rows
        offset = col_index * block_cols - root_row * block_rows
        column_part = lax.dynamic_slice_in_dim(row_full, offset, block_cols, 0)
        return spread(column_part, "row", root_row)

    def backward(row_full):
        partial_value = lax.dot_general(
            shifted,
            row_full,
            (((0,), (0,)), ((), ())),
            precision=lax.Precision.HIGHEST,
            preferred_element_type=jnp.float32,
        )
        return lax.psum(partial_value, "row")

    current_start = lax.all_gather(start_vectors, "row", axis=0, tiled=True)
    for sweep_index in range(OUTER):
        even_cols = current_start
        odd_slab = forward(current_start)
        odd_rows = gather_rows(odd_slab)
        for degree in range(2, FILTER_DEG + 1):
            if degree % 2 == 0:
                even_cols = 2.0 * backward(odd_rows) - even_cols
            else:
                odd_slab = 2.0 * forward(even_cols) - odd_slab
                odd_rows = gather_rows(odd_slab)
        final_cols = to_columns(odd_rows)
        mapped_cols = backward(odd_rows)
        final_slab = lax.dynamic_slice_in_dim(final_cols, row_index * slab_rows, slab_rows, 0)
        mapped_slab = lax.dynamic_slice_in_dim(mapped_cols, row_index * slab_rows, slab_rows, 0)
        gram_part = product(final_slab.T, final_slab)
        cross_part = product(final_slab.T, mapped_slab)
        gram_total = lax.psum(gram_part, ("row", "col"))
        cross_total = lax.psum(cross_part, ("row", "col"))
        gram_matrix = gram_total / total_rows
        cross_terms = cross_total / total_rows
        factor = jnp.linalg.cholesky(gram_matrix)
        basis_cols = tri_solve(factor, final_cols.T).T
        partial_proj = tri_solve(factor, cross_terms)
        projected = tri_solve(factor, partial_proj.T).T
        current_start = basis_cols
    basis_slab = lax.dynamic_slice_in_dim(current_start, row_index * slab_rows, slab_rows, 0)
    residual = tri_solve(factor, mapped_slab.T).T - product(basis_slab, projected)
    return (basis_slab, projected, residual)


def solution(mesh):
    return jax.shard_map(
        on_device,
        mesh=mesh,
        in_specs=(P("row", "col"), P(("col", "row"), None), P()),
        out_specs=(P(("col", "row"), None), P(), P(("col", "row"), None)),
        check_vma=False,
    )
```

profile of v0, /device:TPU:0, one launch (start us, length us, event | category | flops | bytes accessed | tf_op | source)
XLA Modules:
  0.0 1180.5 jit_solution(1612085924572650123)
XLA Ops:
  11.0 8.9 all_gather.15
  19.9 2.1 fusion.159
  22.1 65.2 %reduce-scatter.5.cloned.1.call-done = f32[64,512]{1,0:T(8,128)} async-done(((f32[512,512]{1,0:T(8,128)}), f32[64,512]{1,0:T(8,128)}) %reduce-scatter.5.cloned.1.call-update) | async-done | bytes 131088 | tf_op jit(solution)/shard_map/reduce_scatter | solution.py:12
  87.3 41.6 %all-gather.5.cloned.1.call-done = f32[512,512]{1,0:T(8,128)} async-done(((f32[64,512]{1,0:T(8,128)}), f32[512,512]{1,0:T(8,128)}) %all-gather.5.cloned.1.call-update) | async-done | bytes 1048592 | tf_op jit(solution)/shard_map/all_gather | solution.py:50
  129.0 3.9 fusion.157
  133.2 31.8 %all-reduce.10.cloned.1.call-done = f32[256,512]{0,1:T(8,128)} async-done(((f32[256,512]{0,1:T(8,128)}), f32[256,512]{0,1:T(8,128)}) %all-reduce.10.cloned.1.call-update) | async-done | bytes 524304 | tf_op jit(solution)/shard_map/psum | solution.py:66
  165.0 3.1 fusion.22
  168.2 65.7 %reduce-scatter.7.cloned.1.call-done = f32[64,512]{1,0:T(8,128)} async-done(((f32[512,512]{1,0:T(8,128)}), f32[64,512]{1,0:T(8,128)}) %reduce-scatter.7.cloned.1.call-update) | async-done | bytes 131088 | tf_op jit(solution)/shard_map/reduce_scatter | solution.py:12
  233.9 1.6 multiply_subtract_fusion.1
  235.6 40.5 %all-gather.7.cloned.1.call-done = f32[512,512]{1,0:T(8,128)} async-done(((f32[64,512]{1,0:T(8,128)}), f32[512,512]{1,0:T(8,128)}) %all-gather.7.cloned.1.call-update) | async-done | bytes 1048592 | tf_op jit(solution)/shard_map/all_gather | solution.py:50
  276.1 1.9 dynamic-slice_select_fusion.1
  278.0 32.8 %all-reduce.12.cloned.1.call-done = f32[256,512]{1,0:T(8,128)} async-done(((f32[256,512]{1,0:T(8,128)}), f32[256,512]{1,0:T(8,128)}) %all-reduce.12.cloned.1.call-update) | async-done | bytes 524304 | tf_op jit(solution)/shard_map/psum | solution.py:17
  310.8 3.0 fusion.73
  314.0 133.2 %all-reduce.14.cloned.1.call-done = f32[512,512]{0,1:T(8,128)} async-done(((f32[512,512]{0,1:T(8,128)}), f32[512,512]{0,1:T(8,128)}) %all-reduce.14.cloned.1.call-update) | async-done | bytes 1048592 | tf_op jit(solution)/shard_map/psum | solution.py:85
  447.2 1.3 broadcast_multiply_fusion.2
  448.9 0.9 copy-done.1
  450.0 11.7 cholesky.286
  461.8 9.8 custom-call.36
  472.4 11.7 cholesky.305
  484.1 10.0 custom-call.37
  494.8 11.7 cholesky.326
  507.3 9.8 custom-call.38
  517.7 11.7 cholesky.343
  530.1 1.1 compare_reduce_fusion.6
  533.8 8.5 while.9
  534.5 1.4 bitcast_dynamic-update-slice_fusion.4
  536.6 1.4 bitcast_dynamic-update-slice_fusion.4
  538.8 1.4 bitcast_dynamic-update-slice_fusion.4
  540.9 1.4 bitcast_dynamic-update-slice_fusion.4
  542.3 39.3 %custom-call.39 = f32[4,128,128]{1,2,0:T(8,128)S(1)} custom-call(f32[4,128,128]{2,1,0:T(8,128)S(1)} %get-tuple-element.42), custom_call_target="InvertDiagBlocksLowerTriangular" | custom-call | tf_op jit(solution)/shard_map/jit(_solve_triangular)/triangular_solve | solution.py:25
  584.8 2.1 fusion.35
  586.9 63.4 %reduce-scatter.9.cloned.1.call-done = f32[64,512]{1,0:T(8,128)} async-done(((f32[512,512]{1,0:T(8,128)}), f32[64,512]{1,0:T(8,128)}) %reduce-scatter.9.cloned.1.call-update) | async-done | bytes 131088 | tf_op jit(solution)/shard_map/reduce_scatter | solution.py:12
  650.4 41.6 %all-gather.9.cloned.1.call-done = f32[512,512]{1,0:T(8,128)} async-done(((f32[64,512]{1,0:T(8,128)}), f32[512,512]{1,0:T(8,128)}) %all-gather.9.cloned.1.call-update) | async-done | bytes 1048592 | tf_op jit(solution)/shard_map/all_gather | solution.py:50
  692.0 3.9 fusion.153
  696.0 32.0 %all-reduce.16.cloned.1.call-done = f32[256,512]{0,1:T(8,128)} async-done(((f32[256,512]{0,1:T(8,128)}), f32[256,512]{0,1:T(8,128)}) %all-reduce.16.cloned.1.call-update) | async-done | bytes 524304 | tf_op jit(solution)/shard_map/psum | solution.py:66
  728.1 3.1 fusion.20
  731.2 65.9 %reduce-scatter.11.cloned.1.call-done = f32[64,512]{1,0:T(8,128)} async-done(((f32[512,512]{1,0:T(8,128)}), f32[64,512]{1,0:T(8,128)}) %reduce-scatter.11.cloned.1.call-update) | async-done | bytes 131088 | tf_op jit(solution)/shard_map/reduce_scatter | solution.py:12
  797.1 1.6 multiply_subtract_fusion
  798.8 40.5 %all-gather.11.cloned.1.call-done = f32[512,512]{1,0:T(8,128)} async-done(((f32[64,512]{1,0:T(8,128)}), f32[512,512]{1,0:T(8,128)}) %all-gather.11.cloned.1.call-update) | async-done | bytes 1048592 | tf_op jit(solution)/shard_map/all_gather | solution.py:50
  839.3 3.3 fusion.150
  843.7 35.0 %all-reduce.20.cloned.1.call-done = (f32[256,512]{1,0:T(8,128)}, f32[256,512]{1,0:T(8,128)}) async-done(((f32[256,512]{1,0:T(8,128)}, f32[256,512]{1,0:T(8,128)}), (f32[256,512]{1,0:T(8,128)}, f32[256,512]{1,0:T(8,128)})) %all-reduce.20.cloned.1.call-update) | async-done | bytes 1048592 | tf_op jit(solution)/shard_map/psum | solution.py:17
  878.7 3.0 fusion.78
  881.7 2.9 fusion.75
  884.7 135.1 %all-reduce.18.cloned.1.call-done = (f32[512,512]{0,1:T(8,128)}, f32[512,512]{0,1:T(8,128)}) async-done(((f32[512,512]{0,1:T(8,128)}, f32[512,512]{0,1:T(8,128)}), (f32[512,512]{0,1:T(8,128)}, f32[512,512]{0,1:T(8,128)})) %all-reduce.18.cloned.1.call-update) | async-done | bytes 2097168 | tf_op jit(solution)/shard_map/psum | solution.py:85
  1019.8 2.4 broadcast_multiply_fusion
  1022.9 11.7 cholesky.358
  1035.3 9.8 custom-call.40
  1045.9 12.1 %cholesky.377 = f32[128,128]{1,0:T(8,128)S(1)} custom-call(f32[128,128]{1,0:T(8,128)S(1)} %cholesky.443), custom_call_target="Cholesky" | custom-call | tf_op jit(solution)/shard_map/jit(cholesky)/cholesky | solution.py:89
  1058.7 9.8 custom-call.41
  1069.2 11.7 cholesky.398
  1081.6 9.8 custom-call.42
  1092.0 11.7 cholesky.415
  1107.1 8.5 while.10
  1107.8 1.4 bitcast_dynamic-update-slice_fusion.5
  1109.9 1.4 bitcast_dynamic-update-slice_fusion.5
  1112.0 1.4 bitcast_dynamic-update-slice_fusion.5
  1114.2 1.4 bitcast_dynamic-update-slice_fusion.5
  1115.6 39.5 %custom-call.43 = f32[4,128,128]{1,2,0:T(8,128)S(1)} custom-call(f32[4,128,128]{2,1,0:T(8,128)S(1)} %get-tuple-element.43), custom_call_target="InvertDiagBlocksLowerTriangular" | custom-call | tf_op jit(solution)/shard_map/jit(_solve_triangular)/triangular_solve | solution.py:25
  1162.3 1.0 convolution_subtract_fusion.2
  1163.8 1.5 convolution_subtract_fusion.5
  1167.2 1.0 convolution_subtract_fusion
  1168.6 1.5 convolution_subtract_fusion.4
  1170.6 1.8 convolution_subtract_fusion.16
  1172.5 1.3 copy.21
  (153 shorter events, 32.0 us)
Async XLA Ops:
  7.2 0.7 copy-start.9
  7.2 12.8 %copy-start.10 = (f32[512,256]{1,0:T(8,128)S(1)}, f32[512,256]{1,0:T(8,128)}, u32[]{:S(2)}) copy-start(f32[512,256]{1,0:T(8,128)} %param.8) | copy-start | bytes 1572868
  7.2 80.1 %reduce-scatter.5.cloned.1.call-start = ((), (), s32[]{:S(2)}) async-start(), calls=%async_computation.4 | async-start | bytes 1179648 | tf_op jit(solution)/shard_map/reduce_scatter | solution.py:12
  22.0 107.0 %all-gather.5.cloned.1.call-start = ((), (), s32[]{:S(2)}) async-start(), calls=%async_computation.5 | async-start | bytes 1179648 | tf_op jit(solution)/shard_map/all_gather | solution.py:50
  87.3 77.7 %all-reduce.10.cloned.1.call-start = ((), (), s32[]{:S(2)}) async-start(), calls=%async_computation.6 | async-start | bytes 1048576 | tf_op jit(solution)/shard_map/psum | solution.py:66
  132.9 101.0 %reduce-scatter.7.cloned.1.call-start = ((), (), s32[]{:S(2)}) async-start(), calls=%async_computation.7 | async-start | bytes 1179648 | tf_op jit(solution)/shard_map/reduce_scatter | solution.py:12
  168.1 65.8 %copy-start.6 = (f32[64,512]{1,0:T(8,128)S(1)}, f32[64,512]{1,0:T(8,128)}, u32[]{:S(2)}) copy-start(f32[64,512]{1,0:T(8,128)} %reduce-scatter.5.cloned.1.call-done) | copy-start | bytes 393220
  168.2 107.9 %all-gather.7.cloned.1.call-start = ((), (), s32[]{:S(2)}) async-start(), calls=%async_computation.8 | async-start | bytes 1179648 | tf_op jit(solution)/shard_map/all_gather | solution.py:50
  235.5 75.3 %all-reduce.12.cloned.1.call-start = ((), (), s32[]{:S(2)}) async-start(), calls=%async_computation.9 | async-start | bytes 1048576 | tf_op jit(solution)/shard_map/psum | solution.py:17
  278.0 169.2 %all-reduce.14.cloned.1.call-start = ((), (), s32[]{:S(2)}) async-start(), calls=%async_computation.10 | async-start | bytes 2097152 | tf_op jit(solution)/shard_map/psum | solution.py:85
  313.8 336.5 %reduce-scatter.9.cloned.1.call-start = ((), (), s32[]{:S(2)}) async-start(), calls=%async_computation.11 | async-start | bytes 1179648 | tf_op jit(solution)/shard_map/reduce_scatter | solution.py:12
  448.5 1.2 copy-start.1
  533.7 48.0 %copy-start.4 = (f32[256,512]{1,0:T(8,128)S(1)}, f32[256,512]{1,0:T(8,128)}, u32[]{:S(2)}) copy-start(f32[256,512]{1,0:T(8,128)} %all-reduce.12.cloned.1.call-done) | copy-start | bytes 1572868
  583.6 1.2 copy-start.11
  586.9 105.2 %all-gather.9.cloned.1.call-start = ((), (), s32[]{:S(2)}) async-start(), calls=%async_computation.12 | async-start | bytes 1179648 | tf_op jit(solution)/shard_map/all_gather | solution.py:50
  650.3 77.7 %all-reduce.16.cloned.1.call-start = ((), (), s32[]{:S(2)}) async-start(), calls=%async_computation.13 | async-start | bytes 1048576 | tf_op jit(solution)/shard_map/psum | solution.py:66
  696.0 101.1 %reduce-scatter.11.cloned.1.call-start = ((), (), s32[]{:S(2)}) async-start(), calls=%async_computation.14 | async-start | bytes 1179648 | tf_op jit(solution)/shard_map/reduce_scatter | solution.py:12
  731.2 65.9 %copy-start.5 = (f32[64,512]{1,0:T(8,128)S(1)}, f32[64,512]{1,0:T(8,128)}, u32[]{:S(2)}) copy-start(f32[64,512]{1,0:T(8,128)} %reduce-scatter.9.cloned.1.call-done) | copy-start | bytes 393220
  731.2 108.1 %all-gather.11.cloned.1.call-start = ((), (), s32[]{:S(2)}) async-start(), calls=%async_computation.15 | async-start | bytes 1179648 | tf_op jit(solution)/shard_map/all_gather | solution.py:50
  798.7 80.0 %all-reduce.20.cloned.1.call-start = ((), (), s32[]{:S(2)}) async-start(), calls=%async_computation.17 | async-start | bytes 2097152 | tf_op jit(solution)/shard_map/psum | solution.py:17
  839.3 3.3 copy-start.7
  843.4 176.4 %all-reduce.18.cloned.1.call-start = ((), (), s32[]{:S(2)}) async-start(), calls=%async_computation.16 | async-start | bytes 4194304 | tf_op jit(solution)/shard_map/psum | solution.py:85
  878.7 3.0 copy-start.8
  1019.8 2.4 copy-start
  1155.5 1.3 copy-start.3
  1158.8 2.1 copy-start.2
Sparse Core Ops, SparseCore 0:
  22.1 65.0 reduce-scatter.4
  89.4 39.5 all-gather.4
  133.1 31.9 all-reduce.9
  168.9 64.9 reduce-scatter.6
  236.5 39.5 all-gather.6
  278.8 31.9 all-reduce.11
  316.6 130.5 all-reduce.13
  587.0 63.2 reduce-scatter.8
  652.5 39.5 all-gather.8
  696.1 31.9 all-reduce.15
  732.1 65.0 reduce-scatter.10
  799.7 39.5 all-gather.10
  843.6 35.0 all-reduce.19
  884.7 134.9 all-reduce.17
where the time goes:
time: 1190 us; the launch traced here: 1180 us
  waiting for transfers between devices  825 us (69%)
  other arithmetic  248 us (21%)
  matrix products  53.2 us (4%)
  between operations  22.6 us (2%)
  local copies, waits for them, and re-layouts  22.2 us (2%)
    psum x2, waiting for transfers between devices, on_device(): gram_total = lax.psum(gram_part, ('row', 'col'))  268 us
    reduce_scatter x4, waiting for transfers between devices, scattered(): return lax.psum_scatter(whole, axis, scatter_dimension=0, tiled=True)  260 us
    all_gather x4, waiting for transfers between devices, gather_rows(): return lax.all_gather(slab_part, 'col', axis=0, tiled=True)  164 us
    another operation x29, other arithmetic, on_device(): factor = jnp.linalg.cholesky(gram_matrix)  158 us
    another operation x6, other arithmetic, tri_solve(): return jax.scipy.linalg.solve_triangular(factor, values, lower=True)  79.2 us
    psum x2, waiting for transfers between devices, spread(): return lax.psum(jnp.where(mine, array, jnp.zeros_like(array)), axis)  67.8 us
    psum x2, waiting for transfers between devices, backward(): return lax.psum(partial_value, 'row')  63.9 us
  transfers between devices with their start and end apart: 14, of which 14 were waited for; matrix products, arithmetic and copies ran while one was open for 0% of the time, Pallas kernels for 0%

commit v1 on v0

v1 whole, which is shorter than its diff:
```python
import functools

import jax
import jax.numpy as jnp
from jax import lax
from jax.experimental import pallas as pl
from jax.experimental.pallas import tpu as pltpu
from jax.sharding import PartitionSpec as P

FILTER_DEG = 3
OUTER = 2
PANEL = 8


def product(left, right, precision=lax.Precision.HIGHEST):
    return jnp.dot(left, right, precision=precision, preferred_element_type=jnp.float32)


def contract(left, right, left_dim, right_dim):
    return lax.dot_general(
        left,
        right,
        (((left_dim,), (right_dim,)), ((), ())),
        precision=lax.Precision.HIGHEST,
        preferred_element_type=jnp.float32,
    )


def factor_panel(panel, first):
    rows = panel.shape[0]
    row_at = lax.broadcasted_iota(jnp.int32, panel.shape, 0)
    pivots = jnp.ones((rows, 1), jnp.float32)
    pivot_at = lax.broadcasted_iota(jnp.int32, (rows, 1), 0)
    for step in range(rows):
        column = panel[:, first + step : first + step + 1]
        pivot = column[step : step + 1, :]
        pivots = jnp.where(pivot_at == step, pivot, pivots)
        if step < rows - 1:
            multiplier = column / pivot
            change = multiplier * panel[step : step + 1, :]
            panel = jnp.where(row_at > step, panel - change, panel)
    return panel * lax.rsqrt(pivots)


def factor_kernel(block, gram_ref, inverse_ref, work, tile):
    order = gram_ref.shape[0]
    work[...] = gram_ref[...]
    at_row = lax.broadcasted_iota(jnp.int32, (order, order), 0)
    at_col = lax.broadcasted_iota(jnp.int32, (order, order), 1)
    inverse_ref[...] = (at_row == at_col).astype(jnp.float32)
    unit = (
        lax.broadcasted_iota(jnp.int32, (block, block), 0)
        == lax.broadcasted_iota(jnp.int32, (block, block), 1)
    ).astype(jnp.float32)
    for start in range(0, order, block):
        stop = start + block
        tile[:, :block] = work[start:stop, start:stop]
        tile[:, block:] = unit
        for first in range(0, block, PANEL):
            last = first + PANEL
            done = factor_panel(tile[first:last, :], first)
            tile[first:last, :] = done
            if last < block:
                tile[last:, :] -= contract(done[:, :block], done, 0, 0)[last:, :]
        small = tile[:, block:]
        solved = product(small, inverse_ref[start:stop, :])
        inverse_ref[start:stop, :] = solved
        if stop < order:
            below = contract(work[stop:, start:stop], small, 1, 1)
            work[stop:, stop:] -= contract(below, below, 1, 1)
            inverse_ref[stop:, :] -= product(below, solved)
    inverse_ref[...] = jnp.where(at_row >= at_col, inverse_ref[...], 0.0)


def inverse_factor(gram_matrix):
    order = gram_matrix.shape[0]
    block = min(128, order)
    return pl.pallas_call(
        functools.partial(factor_kernel, block),
        out_shape=jax.ShapeDtypeStruct((order, order), jnp.float32),
        in_specs=[pl.BlockSpec(memory_space=pltpu.VMEM)],
        out_specs=pl.BlockSpec(memory_space=pltpu.VMEM),
        scratch_shapes=[
            pltpu.VMEM((order, order), jnp.float32),
            pltpu.VMEM((block, 2 * block), jnp.float32),
        ],
        cost_estimate=pl.CostEstimate(flops=2 * order**3, bytes_accessed=8 * order**2, transcendentals=order),
    )(gram_matrix)


def on_device(matrix, start_vectors, interval):
    block_rows = matrix.shape[0]
    slab_rows, vectors = start_vectors.shape
    row_count, col_count = lax.axis_size("row"), lax.axis_size("col")
    total_rows = slab_rows * row_count * col_count
    width = vectors // col_count
    row_index = lax.axis_index("row")
    center = 0.5 * (interval[0] + interval[1])
    half_width = 0.5 * (interval[1] - interval[0])

    strip = lax.all_gather(matrix, "col", axis=1, tiled=True)
    global_rows = row_index * block_rows + lax.iota(jnp.int32, block_rows)
    diagonal = global_rows[:, None] == lax.iota(jnp.int32, total_rows)[None, :]
    shifted = jnp.where(diagonal, strip - center, strip) / half_width

    def apply(group):
        return lax.all_gather(product(shifted, group, lax.Precision.HIGH), "row", axis=0, tiled=True)

    def to_group(slab):
        mine = lax.all_to_all(slab, "col", split_axis=1, concat_axis=0, tiled=True)
        every = lax.all_gather(mine.reshape(col_count, slab_rows, width), "row", axis=1)
        return every.reshape(total_rows, width)

    def to_slab(group):
        parts = group.reshape(col_count, row_count, slab_rows, width)
        mine = lax.dynamic_index_in_dim(parts, row_index, 1, keepdims=False)
        return lax.all_to_all(mine.reshape(col_count * slab_rows, width), "col", split_axis=0, concat_axis=1, tiled=True)

    def filtered(group):
        previous, current = group, apply(group)
        for degree in range(2, FILTER_DEG + 1):
            previous, current = current, 2.0 * apply(current) - previous
        return current

    group = to_group(start_vectors)
    inverses = []

    def normalised(slab):
        for inverse in inverses:
            slab = contract(slab, inverse, 1, 1)
        return slab

    for sweep_index in range(OUTER):
        group = filtered(group)
        slab = normalised(to_slab(group))
        if sweep_index == OUTER - 1:
            mapped = normalised(to_slab(apply(group)))
            pair = jnp.concatenate([slab, mapped], axis=1)
            sums = lax.psum(contract(slab, pair, 0, 0), ("row", "col")) / total_rows
            gram, cross = sums[:, :vectors], sums[:, vectors:]
        else:
            gram = lax.psum(contract(slab, slab, 0, 0), ("row", "col")) / total_rows
        inverses.append(inverse_factor(gram))
    inverse = inverses[-1]
    basis = contract(slab, inverse, 1, 1)
    projected = contract(product(inverse, cross), inverse, 1, 1)
    residual = contract(mapped, inverse, 1, 1) - product(basis, projected)
    return basis, projected, residual


def solution(mesh):
    return jax.shard_map(
        on_device,
        mesh=mesh,
        in_specs=(P("row", "col"), P(("col", "row"), None), P()),
        out_specs=(P(("col", "row"), None), P(), P(("col", "row"), None)),
        check_vma=False,
    )
```

time: 1190 us -> 613 us (0.52)
  waiting for transfers between devices: 825 us -> 305 us
  other arithmetic: 248 us -> 10.8 us
  Pallas kernels: 0 us -> 139 us
  blocking collectives: 8.89 us -> 61.2 us
  starting transfers between devices: 0.92 us -> 20.2 us
  matrix products: 53.2 us -> 38.3 us
    reduce_scatter x4 -> x0, waiting for transfers between devices: 260 us -> none  [scattered(): return lax.psum_scatter(whole, axis, scatter_dimension=0, tiled=True)]
    another operation x35 -> x0, other arithmetic: 238 us -> none  [the longest x29 158 us: on_device(): factor = jnp.linalg.cholesky(gram_matrix)]
    psum x6 -> x2, waiting for transfers between devices: 400 us -> 239 us  [the longest x1 134 us: on_device(): sums = lax.psum(contract(slab, pair, 0, 0), ('row', 'col')) / total_rows]
    pallas_call x0 -> x2, Pallas kernels: none -> 139 us  [inverse_factor(): pl.pallas_call(functools.partial(factor_kernel, block), out_shape=jax.Sha...]
    all_gather x4 -> x1, waiting for transfers between devices: 164 us -> 50.6 us  [on_device(): strip = lax.all_gather(matrix, 'col', axis=1, tiled=True)]
    all_gather x1 -> x8, blocking collectives: 8.89 us -> 61.2 us  [the longest x7 51.2 us: apply(): lax.all_gather(product(shifted, group, lax.Precision.HIGH), 'row', axis=0...]
    another operation x47 -> x0, matrix products: 21 us -> none  [the longest x35 17.3 us: tri_solve(): return jax.scipy.linalg.solve_triangular(factor, values, lower=True)]
    all_to_all x0 -> x4, starting transfers between devices: none -> 19.7 us  [the longest x3 12.4 us: to_slab(): lax.all_to_all(mine.reshape(col_count * slab_rows, width), 'col', split_a...]
  transfers between devices with their start and end apart: 14 -> 7, of which waited for: 14 -> 6; matrix products, arithmetic and copies ran while one was open for 0% -> 3% of each run, Pallas kernels for 0% -> 0%
where the time goes in v1:
time: 613 us; the launch traced here: 605 us
  waiting for transfers between devices  305 us (50%)
  Pallas kernels  139 us (23%)
  blocking collectives  61.2 us (10%)
  matrix products  38.3 us (6%)
  starting transfers between devices  20.2 us (3%)
  between operations  17.1 us (3%)
  local copies, waits for them, and re-layouts  12.7 us (2%)
  other arithmetic  10.8 us (2%)
    pallas_call x2, Pallas kernels, inverse_factor(): pl.pallas_call(functools.partial(factor_kernel, block), out_shape=jax.Sha...  139 us
    psum x1, waiting for transfers between devices, on_device(): sums = lax.psum(contract(slab, pair, 0, 0), ('row', 'col')) / total_rows  134 us
    psum x1, waiting for transfers between devices, on_device(): gram = lax.psum(contract(slab, slab, 0, 0), ('row', 'col')) / total_rows  105 us
    all_gather x7, blocking collectives, apply(): lax.all_gather(product(shifted, group, lax.Precision.HIGH), 'row', axis=0...  51.2 us
    all_gather x1, waiting for transfers between devices, on_device(): strip = lax.all_gather(matrix, 'col', axis=1, tiled=True)  50.6 us
    dot_general x9, matrix products, product(): jnp.dot(left, right, precision=precision, preferred_element_type=jnp.floa...  23.1 us
    dot_general x7, matrix products, contract(): lax.dot_general(left, right, (((left_dim,), (right_dim,)), ((), ())), pre...  15.2 us
    all_to_all x3, starting transfers between devices, to_slab(): lax.all_to_all(mine.reshape(col_count * slab_rows, width), 'col', split_a...  12.4 us
  transfers between devices with their start and end apart: 7, of which 6 were waited for; matrix products, arithmetic and copies ran while one was open for 3% of the time, Pallas kernels for 0%

profile of v1, /device:TPU:0, one launch (start us, length us, event | category | flops | bytes accessed | tf_op | source)
XLA Modules:
  0.0 604.5 jit_solution(16130343872022362927)
XLA Ops:
  7.2 0.7 all-gather.3.cloned.1.call-update
  7.9 1.0 copy.11
  8.9 0.8 reshape.56
  9.8 7.3 %all-to-all-start = ((f32[8,1,4096]{2,1,0:T(1,128)}), f32[8,1,4096]{2,1,0:T(1,128)S(1)}, u32[]{:S(2)}, u32[]{:S(2)}) async-start(f32[8,1,4096]{2,1,0:T(1,128)} %reshape.56), calls=%async_computation | async-start | bytes 262144 | tf_op jit(solution)/shard_map/all_to_all | solution.py:110
  17.1 1.3 fusion.18
  21.0 3.4 all-to-all-done
  24.5 0.5 broadcast.20
  25.0 0.9 reduce
  26.2 10.0 %all-gather = f32[8,256,64]{2,0,1:T(8,128)S(1)} all-gather(f32[8,64,64]{2,0,1:T(8,128)S(1)} %copy.12), channel_id=2, replica_groups=mesh['row'=4,'col'=8] {'row'}, dimensions={1}, use_global_device_ids=true | all-gather | bytes 655360 | tf_op jit(solution)/shard_map/all_gather | solution.py:111
  36.2 0.4 copy.13
  36.7 0.2 copy.20
  36.9 50.6 %all-gather.3.cloned.1.call-done = f32[512,2048]{1,0:T(8,128)} async-done(((f32[512,256]{1,0:T(8,128)}), f32[512,2048]{1,0:T(8,128)}) %all-gather.3.cloned.1.call-update) | async-done | bytes 4194320 | tf_op jit(solution)/shard_map/all_gather | solution.py:101
  87.5 2.9 fusion
  90.4 2.0 fusion.19
  92.4 7.1 %all_gather.29 = f32[2048,64]{0,1:T(8,128)S(1)} all-gather(f32[512,64]{0,1:T(8,128)S(1)} %fusion.19), channel_id=1, replica_groups=mesh['row'=4,'col'=8] {'row'}, dimensions={0}, use_global_device_ids=true | all-gather | bytes 655360 | tf_op jit(solution)/shard_map/all_gather | solution.py:107
  99.6 2.0 fusion.20
  101.6 7.3 %all_gather.30 = f32[2048,64]{0,1:T(8,128)S(1)} all-gather(f32[512,64]{0,1:T(8,128)S(1)} %fusion.20), channel_id=1, replica_groups=mesh['row'=4,'col'=8] {'row'}, dimensions={0}, use_global_device_ids=true | all-gather | bytes 655360 | tf_op jit(solution)/shard_map/all_gather | solution.py:107
  108.9 2.0 fusion.6
  110.9 7.3 %all_gather.31 = f32[2048,64]{0,1:T(8,128)S(1)} all-gather(f32[512,64]{0,1:T(8,128)S(1)} %fusion.6), channel_id=1, replica_groups=mesh['row'=4,'col'=8] {'row'}, dimensions={0}, use_global_device_ids=true | all-gather | bytes 655360 | tf_op jit(solution)/shard_map/all_gather | solution.py:107
  118.3 2.0 fusion.21
  120.3 0.7 reshape.52
  121.0 7.6 %all_gather.32 = f32[2048,64]{0,1:T(8,128)S(1)} all-gather(f32[512,64]{0,1:T(8,128)S(1)} %fusion.21), channel_id=1, replica_groups=mesh['row'=4,'col'=8] {'row'}, dimensions={0}, use_global_device_ids=true | all-gather | bytes 655360 | tf_op jit(solution)/shard_map/all_gather | solution.py:107
  128.6 4.2 fusion.22
  132.9 7.3 %all_gather.33 = f32[2048,64]{0,1:T(8,128)S(1)} all-gather(f32[512,64]{0,1:T(8,128)S(1)} %fusion.22), channel_id=1, replica_groups=mesh['row'=4,'col'=8] {'row'}, dimensions={0}, use_global_device_ids=true | all-gather | bytes 655360 | tf_op jit(solution)/shard_map/all_gather | solution.py:107
  140.2 2.0 fusion.3
  142.2 7.3 %all_gather.34 = f32[2048,64]{0,1:T(8,128)S(1)} all-gather(f32[512,64]{0,1:T(8,128)S(1)} %fusion.3), channel_id=1, replica_groups=mesh['row'=4,'col'=8] {'row'}, dimensions={0}, use_global_device_ids=true | all-gather | bytes 655360 | tf_op jit(solution)/shard_map/all_gather | solution.py:107
  149.6 0.3 constant_dynamic-slice_fusion.1
  150.0 0.8 reshape.60
  150.8 3.4 all-to-all-start.2
  154.3 4.2 fusion.25
  158.5 7.3 %all_gather.35 = f32[2048,64]{0,1:T(8,128)S(1)} all-gather(f32[512,64]{0,1:T(8,128)S(1)} %fusion.25), channel_id=1, replica_groups=mesh['row'=4,'col'=8] {'row'}, dimensions={0}, use_global_device_ids=true | all-gather | bytes 655360 | tf_op jit(solution)/shard_map/all_gather | solution.py:107
  165.8 0.7 reshape.53
  166.5 0.9 reduce.2
  167.5 0.2 copy.17
  167.8 2.0 fusion.23
  169.8 0.3 constant_dynamic-slice_fusion
  170.2 0.8 reshape.62
  171.1 5.6 all-to-all-start.3
  176.7 0.7 reshape.51
  177.4 0.3 constant_dynamic-slice_fusion.2
  177.8 0.8 reshape.58
  178.6 5.7 all-to-all-done.3
  184.3 3.4 all-to-all-start.1
  187.7 0.4 all-reduce.5.cloned.1.call-start
  188.2 0.9 reduce.3
  189.2 0.2 copy.19
  189.5 5.7 all-to-all-done.1
  195.2 0.9 reduce.1
  196.2 0.2 copy.15
  196.5 105.1 %all-reduce.3.cloned.1.call-done = f32[512,512]{1,0:T(8,128)} async-done(((f32[512,512]{1,0:T(8,128)}), f32[512,512]{1,0:T(8,128)}) %all-reduce.3.cloned.1.call-update) | async-done | bytes 1048592 | tf_op jit(solution)/shard_map/psum | solution.py:142
  301.6 2.3 broadcast_multiply_fusion.1.gram_ref
  303.9 69.6 %shard_map.58 = f32[512,512]{1,0:T(8,128)} custom-call(f32[512,512]{1,0:T(8,128)} %broadcast_multiply_fusion.1.gram_ref), custom_call_target="tpu_custom_call" | custom-call | flops 268435456 | bytes 2097152 | tf_op jit(solution)/shard_map/pallas_call | solution.py:78
  373.5 2.3 fusion.26
  375.8 2.3 fusion.24
  378.2 3.1 fusion.9
  381.3 133.5 %all-reduce.5.cloned.1.call-done = f32[512,1024]{1,0:T(8,128)} async-done(((f32[512,1024]{1,0:T(8,128)}), f32[512,1024]{1,0:T(8,128)}) %all-reduce.5.cloned.1.call-update) | async-done | bytes 2097168 | tf_op jit(solution)/shard_map/psum | solution.py:139
  514.9 1.8 broadcast_multiply_fusion
  516.6 1.1 slice.18.gram_ref
  517.7 69.9 %shard_map.59 = f32[512,512]{1,0:T(8,128)} custom-call(f32[512,512]{1,0:T(8,128)} %slice.18.gram_ref), custom_call_target="tpu_custom_call" | custom-call | flops 268435456 | bytes 2097152 | tf_op jit(solution)/shard_map/pallas_call | solution.py:78
  587.6 2.4 fusion.29
  590.0 3.1 fusion.1
  593.1 1.1 fusion.27
  594.2 1.9 fusion.28
  596.1 1.4 convolution_subtract_fusion
  (30 shorter events, 1.6 us)
Async XLA Ops:
  7.2 80.3 %all-gather.3.cloned.1.call-start = ((), (), s32[]{:S(2)}) async-start(), calls=%async_computation.4 | async-start | bytes 4718592 | tf_op jit(solution)/shard_map/all_gather | solution.py:101
  9.8 14.7 %all-to-all-start = ((f32[8,1,4096]{2,1,0:T(1,128)}), f32[8,1,4096]{2,1,0:T(1,128)S(1)}, u32[]{:S(2)}, u32[]{:S(2)}) async-start(f32[8,1,4096]{2,1,0:T(1,128)} %reshape.56), calls=%async_computation | async-start | bytes 262144 | tf_op jit(solution)/shard_map/all_to_all | solution.py:110
  90.4 27.9 %copy-start = (f32[512,2048]{1,0:T(8,128)}, f32[512,2048]{1,0:T(8,128)S(1)}, u32[]{:S(2)}) copy-start(f32[512,2048]{1,0:T(8,128)S(1)} %fusion) | copy-start | bytes 12582916
  121.0 19.2 %copy-start.1 = (f32[512,2048]{1,0:T(8,128)S(1)}, f32[512,2048]{1,0:T(8,128)}, u32[]{:S(2)}) copy-start(f32[512,2048]{1,0:T(8,128)} %copy-done) | copy-start | bytes 12582916
  150.8 15.6 %all-to-all-start.2 = ((f32[8,1,4096]{2,1,0:T(1,128)}), f32[8,1,4096]{2,1,0:T(1,128)S(1)}, u32[]{:S(2)}, u32[]{:S(2)}) async-start(f32[8,1,4096]{2,1,0:T(1,128)} %reshape.60), calls=%async_computation.2 | async-start | bytes 262144 | tf_op jit(solution)/shard_map/all_to_all | solution.py:117
  154.2 147.4 %all-reduce.3.cloned.1.call-start = ((), (), s32[]{:S(2)}) async-start(), calls=%async_computation.5 | async-start | bytes 2097152 | tf_op jit(solution)/shard_map/psum | solution.py:142
  171.1 13.3 %all-to-all-start.3 = ((f32[8,1,4096]{2,1,0:T(1,128)}), f32[8,1,4096]{2,1,0:T(1,128)S(1)}, u32[]{:S(2)}, u32[]{:S(2)}) async-start(f32[8,1,4096]{2,1,0:T(1,128)} %reshape.62), calls=%async_computation.3 | async-start | bytes 262144 | tf_op jit(solution)/shard_map/all_to_all | solution.py:117
  184.3 10.8 %all-to-all-start.1 = ((f32[8,1,4096]{2,1,0:T(1,128)}), f32[8,1,4096]{2,1,0:T(1,128)S(1)}, u32[]{:S(2)}, u32[]{:S(2)}) async-start(f32[8,1,4096]{2,1,0:T(1,128)} %reshape.58), calls=%async_computation.1 | async-start | bytes 262144 | tf_op jit(solution)/shard_map/all_to_all | solution.py:117
  187.7 327.1 %all-reduce.5.cloned.1.call-start = ((), (), s32[]{:S(2)}) async-start(), calls=%async_computation.6 | async-start | bytes 4194304 | tf_op jit(solution)/shard_map/psum | solution.py:139
  587.6 5.5 copy-start.2
  594.2 3.3 copy-start.4
  596.1 1.4 copy-start.3
Sparse Core Ops, SparseCore 0:
  10.0 77.3 all-gather.2
  169.9 131.6 all-reduce.2
  381.5 133.3 all-reduce.4
